TPU v7x, 32 devices: a whole 2x2x4 slice. The times are simulated.
32 devices in a mesh: task: 4 (over y, core), col: 8 (over z, x).
Axes of the slice: x: 2, y: 2, z: 4, core: 2. Of those that a mesh axis runs over, the one named last changes fastest.
Arguments:
- deltas: bfloat16 [4, 4096, 14336], P('task', None, 'col'), may hold values from -36 to 36
- sketch: bfloat16 [4, 14336, 256], P('task', 'col'), may hold values from -0.06 to 0.06, as said below
Outputs:
- merged: bfloat16 [4096, 14336], P('task', 'col')
Inputs may be any that keep to these rules, and one draw needn't show every extreme that they name: `sketch`: entries are drawn independently.
All inputs are finite; a program needn't handle non-finite values.
Results may differ from a plain program's by a relative error of at most 0.012.
Values may be sent and summed in bfloat16 or wider, within the bound.
No kernel may reach another device: no remote copies, remote signals or barrier semaphores. Data moves between devices by JAX's collectives and lax.ppermute only.
A program may use at most 192 MiB of HBM per device.

v0:
```python
import jax
import jax.numpy as jnp
from jax import lax
from jax.sharding import PartitionSpec as P


def gram_of(matrix):
    return lax.dot_general(
        matrix,
        matrix,
        (((0,), (0,)), ((), ())),
        precision=lax.Precision.HIGHEST,
        preferred_element_type=jnp.float32,
    )


def solve_rows(product, gram):
    lower = jnp.linalg.cholesky(gram)
    return jax.scipy.linalg.solve_triangular(lower, product.T, lower=True).T.astype(jnp.bfloat16)


def orthonormal(delta, right):
    partial_range = jnp.dot(delta, right, preferred_element_type=jnp.float32)
    summed = lax.psum(partial_range, "col")
    return solve_rows(summed, gram_of(summed))


def shards(deltas, sketch):
    delta = deltas[0]
    basis = orthonormal(delta, sketch[0])
    across = lax.dot_general(
        delta, basis, (((0,), (0,)), ((), ())), preferred_element_type=jnp.float32
    ).astype(jnp.bfloat16)
    basis = orthonormal(delta, across)
    coeffs = lax.dot_general(
        basis, delta, (((0,), (0,)), ((), ())), preferred_element_type=jnp.float32
    ).astype(jnp.bfloat16)
    joined = lax.all_gather(basis, "task", axis=1, tiled=True)
    joint = lax.dot_general(
        joined, joined, (((0,), (0,)), ((), ())), preferred_element_type=jnp.float32
    )
    row_count = joined.shape[0] // lax.axis_size("task")
    joined_rows = lax.dynamic_slice_in_dim(joined, lax.axis_index("task") * row_count, row_count, 0)
    lower = jnp.linalg.cholesky(joint)
    whitened = jax.scipy.linalg.solve_triangular(
        lower, joined_rows.astype(jnp.float32).T, lower=True
    ).T.astype(jnp.bfloat16)
    merged = jnp.dot(
        whitened,
        lax.all_gather(coeffs, "task", axis=0, tiled=True),
        preferred_element_type=jnp.float32,
    )
    return merged.astype(jnp.bfloat16)


def solution(mesh):
    in_specs = (P("task", None, "col"), P("task", "col", None))
    out_specs = P("task", "col")
    return jax.shard_map(shards, mesh=mesh, in_specs=in_specs, out_specs=out_specs, check_vma=False)
```

profile of v0, /device:TPU:0, one launch (start us, length us, event | category | flops | bytes accessed | tf_op | source)
XLA Modules:
  0.0 948.9 jit_solution(13411592491427040166)
XLA Ops:
  7.7 11.1 %fusion.6 = f32[4096,256]{1,0:T(8,128)} fusion(bf16[1,4096,1792]{2,1,0:T(8,128)(2,1)} %param.7, bf16[1,1792,256]{2,1,0:T(8,128)(2,1)S(1)} %copy-done), kind=kOutput, calls=%fused_computation.12 | convolution fusion | flops 3758096384 | bytes 19791872 | tf_op jit(solution)/shard_map/dot_general | solution.py:23
  18.9 159.2 %all-reduce.5.cloned.1.call-done = f32[4096,256]{1,0:T(8,128)} async-done(((f32[4096,256]{1,0:T(8,128)}), f32[4096,256]{1,0:T(8,128)}) %all-reduce.5.cloned.1.call-update) | async-done | bytes 4194320 | tf_op jit(solution)/shard_map/psum | solution.py:24
  178.1 10.2 %fusion.125 = f32[256,256]{1,0:T(8,128)S(1)} fusion(f32[4096,256]{1,0:T(8,128)} %all-reduce.5.cloned.1.call-done), kind=kOutput, calls=%fused_computation.235 | convolution fusion | flops 3221225472 | bytes 4456448 | tf_op jit(solution)/shard_map/dot_general | solution.py:8
  188.5 11.7 %cholesky.671 = f32[128,128]{1,0:T(8,128)S(1)} custom-call(f32[128,128]{1,0:T(8,128)S(1)} %cholesky.721), custom_call_target="Cholesky" | custom-call | tf_op jit(solution)/shard_map/jit(cholesky)/cholesky | solution.py:18
  200.3 9.8 %custom-call.80 = f32[1,128,128]{1,2,0:T(8,128)S(1)} custom-call(f32[1,128,128]{2,1,0:T(8,128)S(1)} %get-tuple-element.110), custom_call_target="InvertDiagBlocksLowerTriangular" | custom-call | tf_op jit(solution)/shard_map/jit(cholesky)/cholesky/custom-call.4 | solution.py:18
  210.6 11.7 %cholesky.681 = f32[128,128]{1,0:T(8,128)S(1)} custom-call(f32[128,128]{1,0:T(8,128)S(1)} %convolution_subtract_fusion.15), custom_call_target="Cholesky" | custom-call | tf_op jit(solution)/shard_map/jit(cholesky)/cholesky | solution.py:18
  224.4 3.9 while.6
  228.2 20.2 %custom-call.81 = f32[2,128,128]{1,2,0:T(8,128)S(1)} custom-call(f32[2,128,128]{2,1,0:T(8,128)S(1)} %get-tuple-element.30), custom_call_target="InvertDiagBlocksLowerTriangular" | custom-call | tf_op jit(solution)/shard_map/jit(_solve_triangular)/triangular_solve | solution.py:19
  248.5 3.7 fusion.22
  252.1 3.5 convolution_subtract_fusion.1
  255.7 2.9 fusion.92
  258.6 17.1 %fusion.8 = f32[4096,256]{0,1:T(8,128)} fusion(bf16[1,4096,1792]{2,1,0:T(8,128)(2,1)} %param.7, bf16[128,4096]{1,0:T(8,128)(2,1)} %fusion.92, f32[128,4096]{1,0:T(8,128)S(1)} %fusion.22), kind=kOutput, calls=%fused_computation.14 | convolution fusion | flops 7520845824 | bytes 22020096 | tf_op jit(solution)/shard_map/dot_general | solution.py:23
  275.8 155.5 %all-reduce.7.cloned.1.call-done = f32[4096,256]{0,1:T(8,128)} async-done(((f32[4096,256]{0,1:T(8,128)}), f32[4096,256]{0,1:T(8,128)}) %all-reduce.7.cloned.1.call-update) | async-done | bytes 4194320 | tf_op jit(solution)/shard_map/psum | solution.py:24
  431.3 12.1 %fusion.126 = f32[256,256]{1,0:T(8,128)S(1)} fusion(f32[4096,256]{0,1:T(8,128)} %all-reduce.7.cloned.1.call-done), kind=kOutput, calls=%fused_computation.236 | convolution fusion | flops 3221225472 | bytes 4456448 | tf_op jit(solution)/shard_map/dot_general | solution.py:8
  443.6 11.7 %cholesky.698 = f32[128,128]{1,0:T(8,128)S(1)} custom-call(f32[128,128]{1,0:T(8,128)S(1)} %cholesky.724), custom_call_target="Cholesky" | custom-call | tf_op jit(solution)/shard_map/jit(cholesky)/cholesky | solution.py:18
  455.4 9.8 %custom-call.82 = f32[1,128,128]{1,2,0:T(8,128)S(1)} custom-call(f32[1,128,128]{2,1,0:T(8,128)S(1)} %get-tuple-element.106), custom_call_target="InvertDiagBlocksLowerTriangular" | custom-call | tf_op jit(solution)/shard_map/jit(cholesky)/cholesky/custom-call.4 | solution.py:18
  465.7 11.7 %cholesky.708 = f32[128,128]{1,0:T(8,128)S(1)} custom-call(f32[128,128]{1,0:T(8,128)S(1)} %convolution_subtract_fusion.14), custom_call_target="Cholesky" | custom-call | tf_op jit(solution)/shard_map/jit(cholesky)/cholesky | solution.py:18
  480.1 3.9 while.7
  483.9 20.1 %custom-call.83 = f32[2,128,128]{1,2,0:T(8,128)S(1)} custom-call(f32[2,128,128]{2,1,0:T(8,128)S(1)} %get-tuple-element.31), custom_call_target="InvertDiagBlocksLowerTriangular" | custom-call | tf_op jit(solution)/shard_map/jit(_solve_triangular)/triangular_solve | solution.py:19
  504.1 3.6 fusion.20
  514.4 10.6 %fusion.15 = bf16[256,1792]{1,0:T(8,128)(2,1)} fusion(bf16[1,4096,1792]{2,1,0:T(8,128)(2,1)} %param.7, bf16[128,4096]{1,0:T(8,128)(2,1)} %copy-done.5, f32[128,4096]{1,0:T(8,128)S(1)} %fusion.20), kind=kOutput, calls=%fused_computation.25 | convolution fusion | flops 3762749440 | bytes 18743296 | tf_op jit(solution)/shard_map/dot_general | solution.py:35
  525.0 46.7 %all-gather.3.cloned.1.call-done = bf16[4096,1024]{0,1:T(8,128)(2,1)} async-done(((bf16[4096,256]{0,1:T(8,128)(2,1)}), bf16[4096,1024]{0,1:T(8,128)(2,1)}) %all-gather.3.cloned.1.call-update) | async-done | bytes 8388624 | tf_op jit(solution)/shard_map/all_gather | solution.py:38
  571.7 16.0 %fusion.127 = f32[1024,1024]{1,0:T(8,128)} fusion(bf16[4096,1024]{0,1:T(8,128)(2,1)} %all-gather.3.cloned.1.call-done), kind=kOutput, calls=%fused_computation.237 | convolution fusion | flops 8589934592 | bytes 12582912 | tf_op jit(solution)/shard_map/dot_general | solution.py:39
  587.7 5.5 copy.7
  593.2 4.5 fusion.11
  599.6 11.7 %cholesky.284 = f32[128,128]{1,0:T(8,128)S(1)} custom-call(f32[128,128]{1,0:T(8,128)S(1)} %cholesky.727), custom_call_target="Cholesky" | custom-call | tf_op jit(solution)/shard_map/jit(cholesky)/cholesky | solution.py:44
  611.4 2.5 cholesky.314
  613.9 9.8 %custom-call.68 = f32[1,128,128]{1,2,0:T(8,128)S(1)} custom-call(f32[1,128,128]{2,1,0:T(8,128)S(1)} %get-tuple-element.102), custom_call_target="InvertDiagBlocksLowerTriangular" | custom-call | tf_op jit(solution)/shard_map/jit(cholesky)/cholesky | solution.py:44
  627.6 11.9 %cholesky.307 = f32[128,128]{1,0:T(8,128)S(1)} custom-call(f32[128,128]{1,0:T(8,128)S(1)} %cholesky.731), custom_call_target="Cholesky" | custom-call | tf_op jit(solution)/shard_map/jit(cholesky)/cholesky | solution.py:44
  641.4 9.8 %custom-call.69 = f32[1,128,128]{1,2,0:T(8,128)S(1)} custom-call(f32[1,128,128]{2,1,0:T(8,128)S(1)} %get-tuple-element.99), custom_call_target="InvertDiagBlocksLowerTriangular" | custom-call | tf_op jit(solution)/shard_map/jit(cholesky)/cholesky | solution.py:44
  654.6 11.7 %cholesky.332 = f32[128,128]{1,0:T(8,128)S(1)} custom-call(f32[128,128]{1,0:T(8,128)S(1)} %cholesky.736), custom_call_target="Cholesky" | custom-call | tf_op jit(solution)/shard_map/jit(cholesky)/cholesky | solution.py:44
  667.6 9.8 %custom-call.70 = f32[1,128,128]{1,2,0:T(8,128)S(1)} custom-call(f32[1,128,128]{2,1,0:T(8,128)S(1)} %get-tuple-element.96), custom_call_target="InvertDiagBlocksLowerTriangular" | custom-call | tf_op jit(solution)/shard_map/jit(cholesky)/cholesky | solution.py:44
  681.0 12.1 %cholesky.543 = f32[128,128]{1,0:T(8,128)S(1)} custom-call(f32[128,128]{1,0:T(8,128)S(1)} %cholesky.741), custom_call_target="Cholesky" | custom-call | tf_op jit(solution)/shard_map/jit(cholesky)/cholesky | solution.py:44
  694.4 9.8 %custom-call.71 = f32[1,128,128]{1,2,0:T(8,128)S(1)} custom-call(f32[1,128,128]{2,1,0:T(8,128)S(1)} %get-tuple-element.93), custom_call_target="InvertDiagBlocksLowerTriangular" | custom-call | tf_op jit(solution)/shard_map/jit(cholesky)/cholesky | solution.py:44
  707.7 11.7 %cholesky.562 = f32[128,128]{1,0:T(8,128)S(1)} custom-call(f32[128,128]{1,0:T(8,128)S(1)} %cholesky.746), custom_call_target="Cholesky" | custom-call | tf_op jit(solution)/shard_map/jit(cholesky)/cholesky | solution.py:44
  720.7 9.9 %custom-call.72 = f32[1,128,128]{1,2,0:T(8,128)S(1)} custom-call(f32[1,128,128]{2,1,0:T(8,128)S(1)} %get-tuple-element.90), custom_call_target="InvertDiagBlocksLowerTriangular" | custom-call | tf_op jit(solution)/shard_map/jit(cholesky)/cholesky | solution.py:44
  734.0 11.7 %cholesky.582 = f32[128,128]{1,0:T(8,128)S(1)} custom-call(f32[128,128]{1,0:T(8,128)S(1)} %cholesky.751), custom_call_target="Cholesky" | custom-call | tf_op jit(solution)/shard_map/jit(cholesky)/cholesky | solution.py:44
  747.0 9.8 %custom-call.73 = f32[1,128,128]{1,2,0:T(8,128)S(1)} custom-call(f32[1,128,128]{2,1,0:T(8,128)S(1)} %get-tuple-element.87), custom_call_target="InvertDiagBlocksLowerTriangular" | custom-call | tf_op jit(solution)/shard_map/jit(cholesky)/cholesky | solution.py:44
  759.8 11.9 %cholesky.602 = f32[128,128]{1,0:T(8,128)S(1)} custom-call(f32[128,128]{1,0:T(8,128)S(1)} %cholesky.756), custom_call_target="Cholesky" | custom-call | tf_op jit(solution)/shard_map/jit(cholesky)/cholesky | solution.py:44
  773.0 9.8 %custom-call.84 = f32[1,128,128]{1,2,0:T(8,128)S(1)} custom-call(f32[1,128,128]{2,1,0:T(8,128)S(1)} %get-tuple-element.84), custom_call_target="InvertDiagBlocksLowerTriangular" | custom-call | tf_op jit(solution)/shard_map/jit(cholesky)/cholesky/custom-call.4 | solution.py:44
  785.4 11.7 %cholesky.616 = f32[128,128]{1,0:T(8,128)S(1)} custom-call(f32[128,128]{1,0:T(8,128)S(1)} %convolution_subtract_fusion.13), custom_call_target="Cholesky" | custom-call | tf_op jit(solution)/shard_map/jit(cholesky)/cholesky | solution.py:44
  803.2 4.8 select_select_fusion
  808.0 23.0 %while.5 = (s32[]{:T(128)}, f32[1024,1024]{1,0:T(8,128)}, s32[8,2]{0,1:T(2,128)S(1)}, f32[8,128,128]{2,1,0:T(8,128)S(1)}, s32[]{:T(128)}) while((s32[]{:T(128)}, f32[1024,1024]{1,0:T(8,128)}, s32[8,2]{0,1:T(2,128)S(1)}, f32[8,128,128]{2,1,0:T(8,128)S(1)}, s32[]{:T(128)}) %tuple.98), condition=%wide.while_cond.1, body=%wide.while_body.1.sunk | while | flops 2 | bytes 131181 | solution.py:45
  831.1 79.0 %custom-call.74 = f32[8,128,128]{1,2,0:T(8,128)S(1)} custom-call(f32[8,128,128]{2,1,0:T(8,128)S(1)} %get-tuple-element.23), custom_call_target="InvertDiagBlocksLowerTriangular" | custom-call | tf_op jit(solution)/shard_map/jit(_solve_triangular)/triangular_solve | solution.py:45
  923.4 2.6 convolution_subtract_fusion.4
  926.9 2.8 convolution_subtract_fusion.3
  930.4 3.4 convolution_subtract_fusion.5
  934.5 7.6 convolution_convert_fusion
  (145 shorter events, 92.2 us)
Async XLA Ops:
  6.5 1.2 copy-start
  6.5 171.6 %all-reduce.5.cloned.1.call-start = ((), (), s32[]{:S(2)}) async-start(), calls=%async_computation | async-start | bytes 8388608 | tf_op jit(solution)/shard_map/psum | solution.py:24
  18.9 412.4 %all-reduce.7.cloned.1.call-start = ((), (), s32[]{:S(2)}) async-start(), calls=%async_computation.1 | async-start | bytes 8388608 | tf_op jit(solution)/shard_map/psum | solution.py:24
  248.5 3.7 copy-start.2
  275.8 295.9 %all-gather.3.cloned.1.call-start = ((), (), s32[]{:S(2)}) async-start(), calls=%async_computation.2 | async-start | bytes 10485760 | tf_op jit(solution)/shard_map/all_gather | solution.py:38
  504.1 3.7 copy-start.3
  511.6 1.1 copy-start.5
  514.3 420.2 %all-gather.5.cloned.1.call-start = ((), (), s32[]{:S(2)}) async-start(), calls=%async_computation.3 | async-start | bytes 4587520 | tf_op jit(solution)/shard_map/all_gather | solution.py:50
  597.6 2.0 copy-start.4
  934.5 7.6 copy-start.1
Sparse Core Ops, SparseCore 0:
  19.0 159.0 all-reduce.4
  275.9 155.3 all-reduce.6
  514.4 57.2 all-gather.2
  573.1 31.5 all-gather.4
where the time goes:
time: 956 us; the launch traced here: 949 us
  other arithmetic  374 us (39%)
  waiting for transfers between devices  361 us (38%)
  matrix products  148 us (15%)
  local copies, waits for them, and re-layouts  44.1 us (5%)
  between operations  21.2 us (2%)
    psum x2, waiting for transfers between devices, orthonormal(): summed = lax.psum(partial_range, 'col')  315 us
    another operation x31, other arithmetic, shards(): lower = jnp.linalg.cholesky(joint)  173 us
    another operation x3, other arithmetic, shards(): jax.scipy.linalg.solve_triangular(lower, joined_rows.astype(jnp.float32)....  83.8 us
    another operation x13, other arithmetic, solve_rows(): lower = jnp.linalg.cholesky(gram)  68.6 us
    all_gather x1, waiting for transfers between devices, shards(): joined = lax.all_gather(basis, 'task', axis=1, tiled=True)  46.7 us
    another operation x5, other arithmetic, solve_rows(): jax.scipy.linalg.solve_triangular(lower, product.T, lower=True)  40.4 us
    dot_general x2, matrix products, orthonormal(): partial_range = jnp.dot(delta, right, preferred_element_type=jnp.float32)  28.3 us
    another operation x14, matrix products, shards(): lower = jnp.linalg.cholesky(joint)  23.1 us
  transfers between devices with their start and end apart: 4, of which 3 were waited for; matrix products, arithmetic and copies ran while one was open for 39% of the time, Pallas kernels for 0%

commit v1 on v0

v1 whole, which is shorter than its diff:
```python
import jax
import jax.numpy as jnp
from jax import lax
from jax.experimental import pallas as pl
from jax.experimental.pallas import tpu as pltpu
from jax.sharding import PartitionSpec as P

BLOCK = 128
SUB = 8
CHUNK = 256


def dot_exact(lhs, rhs):
    return jnp.dot(lhs, rhs, precision=lax.Precision.HIGHEST, preferred_element_type=jnp.float32)


def inverse_factor_block(block):
    groups = BLOCK // SUB
    rows = lax.broadcasted_iota(jnp.int32, (SUB, BLOCK), 0)
    lanes = lax.broadcasted_iota(jnp.int32, (SUB, BLOCK), 1)
    left = [block[g * SUB : (g + 1) * SUB, :] for g in range(groups)]
    right = [(lanes == rows + g * SUB).astype(jnp.float32) for g in range(groups)]
    for j in range(BLOCK):
        home, sub = divmod(j, SUB)
        column = jnp.broadcast_to(left[home][:, j : j + 1], (SUB, BLOCK))
        inverse = 1.0 / column[sub : sub + 1, :]
        row_left = left[home][sub : sub + 1, :] * inverse
        row_right = right[home][sub : sub + 1, :] * inverse
        for g in range(home, groups):
            if g == home:
                factor = jnp.where(rows > sub, column, 0.0)
            else:
                factor = jnp.broadcast_to(left[g][:, j : j + 1], (SUB, BLOCK))
            left[g] = left[g] - factor * row_left
            right[g] = right[g] - factor * row_right
    scaled = []
    for g in range(groups):
        pivot = jnp.sum(jnp.where(lanes == rows + g * SUB, left[g], 0.0), axis=1, keepdims=True)
        scaled.append(right[g] * lax.rsqrt(pivot))
    return jnp.concatenate(scaled, axis=0)


def eliminate(out_ref, inverse, lo):
    size = out_ref.shape[0]
    hi = lo + BLOCK
    if lo:
        out_ref[lo:hi, :lo] = dot_exact(inverse, out_ref[lo:hi, :lo])
    out_ref[lo:hi, lo:hi] = inverse
    if hi == size:
        return
    panel = dot_exact(inverse, out_ref[lo:hi, hi:])
    out_ref[lo:hi, hi:] = jnp.zeros_like(panel)
    turned = panel.T
    for top in range(hi, size, CHUNK):
        end = min(top + CHUNK, size)
        part = turned[top - hi : end - hi, :]
        out_ref[top:end, top:] -= dot_exact(part, panel[:, top - hi :])
        if lo:
            out_ref[top:end, :lo] -= dot_exact(part, out_ref[lo:hi, :lo])
        out_ref[top:end, lo:hi] = -dot_exact(part, inverse)


def inverse_factor_kernel(gram_ref, out_ref, block_ref):
    steps = gram_ref.shape[0] // BLOCK
    out_ref[...] = gram_ref[...]
    block_ref[...] = gram_ref[:BLOCK, :BLOCK]

    @pl.loop(0, steps)
    def _(step):
        block_ref[...] = inverse_factor_block(block_ref[...])
        for k in range(steps):

            @pl.when(step == k)
            def _():
                eliminate(out_ref, block_ref[...], k * BLOCK)
                if k + 1 < steps:
                    end = (k + 2) * BLOCK
                    block_ref[...] = out_ref[end - BLOCK : end, end - BLOCK : end]


def inverse_factor(gram):
    return pl.pallas_call(
        inverse_factor_kernel,
        out_shape=jax.ShapeDtypeStruct(gram.shape, jnp.float32),
        scratch_shapes=[pltpu.VMEM((BLOCK, BLOCK), jnp.float32)],
        compiler_params=pltpu.CompilerParams(vmem_limit_bytes=48 * 1024 * 1024),
        name="inverse_factor",
    )(gram)


def summed(partial):
    devices = lax.axis_size("col")
    rows = partial.shape[0] // devices
    parts = lax.all_to_all(partial.astype(jnp.bfloat16), "col", 0, 0, tiled=True)
    parts = parts.reshape(devices, rows, partial.shape[1])
    return jnp.sum(parts.astype(jnp.float32), axis=0).astype(jnp.bfloat16)


def product(lhs, rhs, contract):
    return lax.dot_general(lhs, rhs, (contract, ((), ())), preferred_element_type=jnp.float32)


ROWS = ((0,), (0,))
INNER = ((1,), (0,))


def shards(deltas, sketch):
    delta = deltas[0]
    first = lax.all_gather(summed(product(delta, sketch[0], INNER)), "col", axis=0, tiled=True)
    norms = jnp.sum(jnp.square(first.astype(jnp.float32)), axis=0, keepdims=True)
    across = (product(delta, first, ROWS) * lax.rsqrt(norms)).astype(jnp.bfloat16)
    tasks = lax.axis_size("task")
    ranges = lax.all_gather(summed(product(delta, across, INNER)), ("task", "col"), axis=0, tiled=True)
    ranges = ranges.reshape(tasks, delta.shape[0], -1)
    ranged = lax.dynamic_index_in_dim(ranges, lax.axis_index("task"), 0, keepdims=False)
    inverse = inverse_factor(product(ranged, ranged, ROWS))
    coeffs = dot_exact(inverse, product(ranged, delta, ROWS)).astype(jnp.bfloat16)
    stacked = lax.all_gather(coeffs, "task", axis=0, tiled=True)
    joined = jnp.concatenate([ranges[t] for t in range(tasks)], axis=1)
    joint = inverse_factor(product(joined, joined, ROWS))
    row_count = joined.shape[0] // tasks
    joined_rows = lax.dynamic_slice_in_dim(joined, lax.axis_index("task") * row_count, row_count, 0)
    whitened = lax.dot_general(
        joined_rows.astype(jnp.float32),
        joint,
        (((1,), (1,)), ((), ())),
        precision=lax.Precision.HIGHEST,
        preferred_element_type=jnp.float32,
    ).astype(jnp.bfloat16)
    return product(whitened, stacked, INNER).astype(jnp.bfloat16)


def solution(mesh):
    in_specs = (P("task", None, "col"), P("task", "col", None))
    out_specs = P("task", "col")
    return jax.shard_map(shards, mesh=mesh, in_specs=in_specs, out_specs=out_specs, check_vma=False)
```

time: 956 us -> 478 us (0.50)
  other arithmetic: 374 us -> 5.59 us
  waiting for transfers between devices: 361 us -> 131 us
  Pallas kernels: 0 us -> 138 us
  blocking collectives: 0 us -> 106 us
  matrix products: 148 us -> 64.8 us
  local copies, waits for them, and re-layouts: 44.1 us -> 17.3 us
    another operation x52 -> x0, other arithmetic: 366 us -> none  [the longest x31 173 us: shards(): lower = jnp.linalg.cholesky(joint)]
    psum x2 -> x0, waiting for transfers between devices: 315 us -> none  [orthonormal(): summed = lax.psum(partial_range, 'col')]
    pallas_call x0 -> x2, Pallas kernels: none -> 138 us  [inverse_factor(): pl.pallas_call(inverse_factor_kernel, out_shape=jax.ShapeDtypeStruct(gram...]
    all_to_all x0 -> x2, blocking collectives: none -> 106 us  [summed(): lax.all_to_all(partial.astype(jnp.bfloat16), 'col', 0, 0, tiled=True)]
    all_gather x2 -> x3, waiting for transfers between devices: 46.7 us -> 131 us  [the longest x1 82.7 us: shards(): lax.all_gather(summed(product(delta, across, INNER)), ('task', 'col'), ax...]
    another operation x39 -> x0, matrix products: 62.7 us -> none  [the longest x14 23.1 us: shards(): lower = jnp.linalg.cholesky(joint)]
    another operation x53 -> x0, local copies, waits for them, and re-layouts: 33.3 us -> none
    dot_general x7 -> x8, matrix products: 84.8 us -> 64.8 us  [the longest x6 54 us: product(): lax.dot_general(lhs, rhs, (contract, ((), ())), preferred_element_type=jn...]
  transfers between devices with their start and end apart: 4 -> 3, of which waited for: 3 -> 2; matrix products, arithmetic and copies ran while one was open for 39% -> 5% of each run, Pallas kernels for 0% -> 24%
where the time goes in v1:
time: 478 us; the launch traced here: 476 us
  Pallas kernels  138 us (29%)
  waiting for transfers between devices  131 us (27%)
  blocking collectives  106 us (22%)
  matrix products  64.8 us (14%)
  local copies, waits for them, and re-layouts  17.3 us (4%)
  between operations  13.4 us (3%)
  other arithmetic  5.59 us (1%)
    pallas_call x2, Pallas kernels, inverse_factor(): pl.pallas_call(inverse_factor_kernel, out_shape=jax.ShapeDtypeStruct(gram...  138 us
    all_to_all x2, blocking collectives, summed(): lax.all_to_all(partial.astype(jnp.bfloat16), 'col', 0, 0, tiled=True)  106 us
    all_gather x1, waiting for transfers between devices, shards(): lax.all_gather(summed(product(delta, across, INNER)), ('task', 'col'), ax...  82.7 us
    dot_general x6, matrix products, product(): lax.dot_general(lhs, rhs, (contract, ((), ())), preferred_element_type=jn...  54 us
    all_gather x1, waiting for transfers between devices, shards(): lax.all_gather(summed(product(delta, sketch[0], INNER)), 'col', axis=0, t...  48.2 us
    reshape x1, local copies, waits for them, and re-layouts, shards(): ranges = ranges.reshape(tasks, delta.shape[0], -1)  12 us
  transfers between devices with their start and end apart: 3, of which 2 were waited for; matrix products, arithmetic and copies ran while one was open for 5% of the time, Pallas kernels for 24%

profile of v1, /device:TPU:0, one launch (start us, length us, event | category | flops | bytes accessed | tf_op | source)
XLA Modules:
  0.0 476.4 jit_solution(13112438487963330882)
XLA Ops:
  6.5 0.0 copy-start
  6.5 0.0 all-gather.4.cloned.1.call-start
  6.5 1.2 copy-done
  7.7 9.2 %fusion.8 = bf16[4096,256]{1,0:T(8,128)(2,1)S(1)} fusion(bf16[1,4096,1792]{2,1,0:T(8,128)(2,1)} %param.2, bf16[1,1792,256]{2,1,0:T(8,128)(2,1)S(1)} %copy-done), kind=kOutput, calls=%fused_computation.9 | convolution fusion | flops 3759144960 | bytes 17694720 | tf_op jit(solution)/shard_map/dot_general | solution.py:100
  16.9 55.3 %all_to_all.18 = bf16[8,512,256]{2,1,0:T(8,128)(2,1)S(1)} all-to-all(bf16[8,512,256]{2,1,0:T(8,128)(2,1)S(1)} %bitcast.53), channel_id=1, replica_groups=mesh['task'=4,'col'=8] {'col'}, dimensions={0} | all-to-all | bytes 4194304 | tf_op jit(solution)/shard_map/all_to_all | solution.py:94
  72.2 1.0 reduce_sum.33
  73.2 0.0 all-gather.4.cloned.1.call-update
  73.3 0.0 all-gather.6.cloned.1.call-start
  73.3 48.2 %all-gather.4.cloned.1.call-done = bf16[4096,256]{1,0:T(8,128)(2,1)} async-done(((bf16[512,256]{1,0:T(8,128)(2,1)}), bf16[4096,256]{1,0:T(8,128)(2,1)}) %all-gather.4.cloned.1.call-update) | async-done | bytes 2097168 | tf_op jit(solution)/shard_map/all_gather | solution.py:109
  121.5 2.2 multiply_reduce_fusion
  123.7 15.5 %fusion.11 = bf16[256,4096]{1,0:T(8,128)(2,1)S(1)} fusion(bf16[1,4096,1792]{2,1,0:T(8,128)(2,1)} %param.2, bf16[4096,256]{1,0:T(8,128)(2,1)} %all-gather.4.cloned.1.call-done, f32[256]{0:T(256)S(1)} %rsqrt.8), kind=kOutput, calls=%fused_computation.10 | convolution fusion | flops 7518158848 | bytes 18875392 | tf_op jit(solution)/shard_map/dot_general | solution.py:100
  139.2 0.2 copy.15
  139.4 50.7 %all_to_all.19 = bf16[8,512,256]{1,2,0:T(8,128)(2,1)S(1)} all-to-all(bf16[8,512,256]{1,2,0:T(8,128)(2,1)S(1)} %bitcast.51), channel_id=1, replica_groups=mesh['task'=4,'col'=8] {'col'}, dimensions={0} | all-to-all | bytes 4194304 | tf_op jit(solution)/shard_map/all_to_all | solution.py:94
  190.1 1.0 reduce_sum.35
  191.1 0.0 all-gather.6.cloned.1.call-update
  191.1 0.4 all-gather.8.cloned.1.call-start
  191.6 82.7 %all-gather.6.cloned.1.call-done = bf16[16384,256]{0,1:T(8,128)(2,1)} async-done(((bf16[512,256]{0,1:T(8,128)(2,1)}), bf16[16384,256]{0,1:T(8,128)(2,1)}) %all-gather.6.cloned.1.call-update) | async-done | bytes 8388624 | tf_op jit(solution)/shard_map/all_gather | solution.py:113
  274.2 12.0 %copy.11 = bf16[16384,256]{1,0:T(8,128)(2,1)} copy(bf16[16384,256]{0,1:T(8,128)(2,1)} %all-gather.6.cloned.1.call-done) | data formatting | bytes 16777216 | tf_op jit(solution)/shard_map/reshape | solution.py:114
  286.2 3.0 fusion.21.gram_ref
  289.2 8.5 %fusion = f32[256,1792]{1,0:T(8,128)S(1)} fusion(bf16[1,4096,1792]{2,1,0:T(8,128)(2,1)} %param.2, bf16[4,4096,256]{2,1,0:T(8,128)(2,1)} %bitcast.50, s32[]{:T(128)S(6)} %select_n.8), kind=kOutput, calls=%fused_computation | convolution fusion | flops 3758096384 | bytes 18612228 | tf_op jit(solution)/shard_map/dot_general | solution.py:100
  297.7 22.3 %inverse_factor.3 = f32[256,256]{1,0:T(8,128)S(1)} custom-call(f32[256,256]{1,0:T(8,128)S(1)} %fusion.21.gram_ref), custom_call_target="tpu_custom_call" | custom-call | tf_op jit(solution)/shard_map/inverse_factor/pallas_call | solution.py:82
  320.0 2.6 convolution_convert_fusion.1
  322.6 0.0 all-gather.8.cloned.1.call-update
  322.6 3.9 fusion.32
  326.6 1.3 pad_maximum_fusion
  327.9 10.4 %fusion.33.gram_ref = f32[1024,1024]{1,0:T(8,128)} fusion(bf16[4096,1024]{0,1:T(8,128)(2,1)S(1)} %pad_maximum_fusion), kind=kOutput, calls=%fused_computation.30 | convolution fusion | flops 8589934592 | bytes 12582912 | tf_op jit(solution)/shard_map/dot_general | solution.py:100
  338.3 115.5 %inverse_factor.2 = f32[1024,1024]{1,0:T(8,128)S(1)} custom-call(f32[1024,1024]{1,0:T(8,128)} %fusion.33.gram_ref), custom_call_target="tpu_custom_call" | custom-call | tf_op jit(solution)/shard_map/inverse_factor/pallas_call | solution.py:82
  453.9 8.2 %fusion.24 = bf16[1024,1024]{1,0:T(8,128)(2,1)S(1)} fusion(f32[1024,1024]{1,0:T(8,128)S(1)} %inverse_factor.2, bf16[4096,1024]{0,1:T(8,128)(2,1)S(1)} %pad_maximum_fusion, s32[]{:T(128)S(6)} %select_n.7), kind=kOutput, calls=%fused_computation.21 | convolution fusion | flops 12884901888 | bytes 8388612 | tf_op jit(solution)/shard_map/dot_general | solution.py:123
  462.1 0.0 all-gather.8.cloned.1.call-done
  462.1 0.0 copy-start.1
  462.2 7.5 %convolution_convert_fusion = bf16[1024,1792]{1,0:T(8,128)(2,1)} fusion(bf16[1024,1792]{1,0:T(8,128)(2,1)} %all-gather.8.cloned.1.call-done, bf16[1024,1024]{1,0:T(8,128)(2,1)S(1)} %fusion.24), kind=kOutput, calls=%fused_computation.12 | convolution fusion | flops 3759931392 | bytes 9437184 | tf_op jit(solution)/shard_map/dot_general | solution.py:100
  469.7 0.0 copy-done.1
  (1 shorter events, 0.0 us)
Async XLA Ops:
  6.5 1.2 copy-start
  6.5 115.0 %all-gather.4.cloned.1.call-start = ((), (), s32[]{:S(2)}) async-start(), calls=%async_computation.2 | async-start | bytes 2359296 | tf_op jit(solution)/shard_map/all_gather | solution.py:109
  73.3 201.0 %all-gather.6.cloned.1.call-start = ((), (), s32[]{:S(2)}) async-start(), calls=%async_computation.3 | async-start | bytes 8650752 | tf_op jit(solution)/shard_map/all_gather | solution.py:113
  191.1 271.0 %all-gather.8.cloned.1.call-start = ((), (), s32[]{:S(2)}) async-start(), calls=%async_computation.4 | async-start | bytes 4587520 | tf_op jit(solution)/shard_map/all_gather | solution.py:118
  462.1 7.5 %copy-start.1 = (bf16[1,1792,256]{2,1,0:T(8,128)(2,1)S(1)}, bf16[1,1792,256]{2,1,0:T(8,128)(2,1)}, u32[]{:S(2)}) copy-start(bf16[1,1792,256]{2,1,0:T(8,128)(2,1)} %param.3) | copy-start | bytes 2752516
Sparse Core Ops, SparseCore 0:
  73.4 48.1 all-gather.3
  191.3 82.9 all-gather.5
  322.7 29.6 all-gather.7

commit v2 on v1

--- a/solution.py
+++ b/solution.py
@@ -7,6 +7,7 @@
 
 BLOCK = 128
 SUB = 8
+STRIDE = 4
 CHUNK = 256
 
 
@@ -20,19 +21,34 @@
     lanes = lax.broadcasted_iota(jnp.int32, (SUB, BLOCK), 1)
     left = [block[g * SUB : (g + 1) * SUB, :] for g in range(groups)]
     right = [(lanes == rows + g * SUB).astype(jnp.float32) for g in range(groups)]
-    for j in range(BLOCK):
-        home, sub = divmod(j, SUB)
-        column = jnp.broadcast_to(left[home][:, j : j + 1], (SUB, BLOCK))
-        inverse = 1.0 / column[sub : sub + 1, :]
-        row_left = left[home][sub : sub + 1, :] * inverse
-        row_right = right[home][sub : sub + 1, :] * inverse
-        for g in range(home, groups):
-            if g == home:
-                factor = jnp.where(rows > sub, column, 0.0)
-            else:
-                factor = jnp.broadcast_to(left[g][:, j : j + 1], (SUB, BLOCK))
-            left[g] = left[g] - factor * row_left
-            right[g] = right[g] - factor * row_right
+    for start in range(0, BLOCK, STRIDE):
+        home, base = divmod(start, SUB)
+
+        def columns_of(g):
+            part = left[g]
+            return [jnp.broadcast_to(part[:, j : j + 1], (SUB, BLOCK)) for j in range(start, start + STRIDE)]
+
+        columns = columns_of(home)
+        pivots = []
+        for k in range(STRIDE):
+            sub = base + k
+            inverse = 1.0 / columns[k][sub : sub + 1, :]
+            row_left = left[home][sub : sub + 1, :] * inverse
+            row_right = right[home][sub : sub + 1, :] * inverse
+            ahead = [columns[m][sub : sub + 1, :] * inverse for m in range(k + 1, STRIDE)]
+            pivots.append((row_left, row_right, ahead))
+            factor = jnp.where(rows > sub, columns[k], 0.0)
+            left[home] = left[home] - factor * row_left
+            right[home] = right[home] - factor * row_right
+            for m in range(k + 1, STRIDE):
+                columns[m] = columns[m] - factor * ahead[m - k - 1]
+        for g in range(home + 1, groups):
+            columns = columns_of(g)
+            for k, (row_left, row_right, ahead) in enumerate(pivots):
+                left[g] = left[g] - columns[k] * row_left
+                right[g] = right[g] - columns[k] * row_right
+                for m in range(k + 1, STRIDE):
+                    columns[m] = columns[m] - columns[k] * ahead[m - k - 1]
     scaled = []
     for g in range(groups):
         pivot = jnp.sum(jnp.where(lanes == rows + g * SUB, left[g], 0.0), axis=1, keepdims=True)
@@ -109,16 +125,13 @@
     first = lax.all_gather(summed(product(delta, sketch[0], INNER)), "col", axis=0, tiled=True)
     norms = jnp.sum(jnp.square(first.astype(jnp.float32)), axis=0, keepdims=True)
     across = (product(delta, first, ROWS) * lax.rsqrt(norms)).astype(jnp.bfloat16)
-    tasks = lax.axis_size("task")
-    ranges = lax.all_gather(summed(product(delta, across, INNER)), ("task", "col"), axis=0, tiled=True)
-    ranges = ranges.reshape(tasks, delta.shape[0], -1)
-    ranged = lax.dynamic_index_in_dim(ranges, lax.axis_index("task"), 0, keepdims=False)
+    ranged = lax.all_gather(summed(product(delta, across, INNER)), "col", axis=0, tiled=True)
+    joined = lax.all_gather(ranged, "task", axis=1, tiled=True)
     inverse = inverse_factor(product(ranged, ranged, ROWS))
     coeffs = dot_exact(inverse, product(ranged, delta, ROWS)).astype(jnp.bfloat16)
     stacked = lax.all_gather(coeffs, "task", axis=0, tiled=True)
-    joined = jnp.concatenate([ranges[t] for t in range(tasks)], axis=1)
     joint = inverse_factor(product(joined, joined, ROWS))
-    row_count = joined.shape[0] // tasks
+    row_count = joined.shape[0] // lax.axis_size("task")
     joined_rows = lax.dynamic_slice_in_dim(joined, lax.axis_index("task") * row_count, row_count, 0)
     whitened = lax.dot_general(
         joined_rows.astype(jnp.float32),

time: 478 us -> 405 us (0.85)
  Pallas kernels: 138 us -> 74.6 us
  local copies, waits for them, and re-layouts: 17.3 us -> 1.38 us
  matrix products: 64.8 us -> 70.8 us
    pallas_call x2, Pallas kernels: 138 us -> 74.6 us  [inverse_factor(): pl.pallas_call(inverse_factor_kernel, out_shape=jax.ShapeDtypeStruct(gram...]
    reshape x1 -> x0, local copies, waits for them, and re-layouts: 12 us -> none  [shards(): ranges = ranges.reshape(tasks, delta.shape[0], -1)]
    dot_general x6, matrix products: 54 us -> 58.9 us  [product(): lax.dot_general(lhs, rhs, (contract, ((), ())), preferred_element_type=jn...]
    all_gather x1 -> x2, waiting for transfers between devices: 82.7 us -> 83.7 us  [the longest x1 49.3 us: shards(): lax.all_gather(summed(product(delta, across, INNER)), 'col', axis=0, tile...]
  transfers between devices with their start and end apart: 3 -> 4, of which waited for: 2 -> 3; matrix products, arithmetic and copies ran while one was open for 5% -> 10% of each run, Pallas kernels for 24% -> 19%
where the time goes in v2:
time: 405 us; the launch traced here: 403 us
  waiting for transfers between devices  132 us (33%)
  blocking collectives  106 us (26%)
  Pallas kernels  74.6 us (18%)
  matrix products  70.8 us (17%)
  between operations  13.4 us (3%)
  other arithmetic  4.25 us (1%)
    all_to_all x2, blocking collectives, summed(): lax.all_to_all(partial.astype(jnp.bfloat16), 'col', 0, 0, tiled=True)  106 us
    pallas_call x2, Pallas kernels, inverse_factor(): pl.pallas_call(inverse_factor_kernel, out_shape=jax.ShapeDtypeStruct(gram...  74.6 us
    dot_general x6, matrix products, product(): lax.dot_general(lhs, rhs, (contract, ((), ())), preferred_element_type=jn...  58.9 us
    all_gather x1, waiting for transfers between devices, shards(): lax.all_gather(summed(product(delta, across, INNER)), 'col', axis=0, tile...  49.3 us
    all_gather x1, waiting for transfers between devices, shards(): lax.all_gather(summed(product(delta, sketch[0], INNER)), 'col', axis=0, t...  48.2 us
    all_gather x1, waiting for transfers between devices, shards(): joined = lax.all_gather(ranged, 'task', axis=1, tiled=True)  34.4 us
    dot_general x1, matrix products, shards(): lax.dot_general(joined_rows.astype(jnp.float32), joint, (((1,), (1,)), ((...  9.28 us
  transfers between devices with their start and end apart: 4, of which 3 were waited for; matrix products, arithmetic and copies ran while one was open for 10% of the time, Pallas kernels for 19%

profile of v2, /device:TPU:0, one launch (start us, length us, event | category | flops | bytes accessed | tf_op | source)
XLA Modules:
  0.0 402.8 jit_solution(16144767481188684455)
XLA Ops:
  6.5 0.0 copy-start
  6.5 0.0 all-gather.5.cloned.1.call-start
  6.5 1.2 copy-done
  7.7 9.2 %fusion.8 = bf16[4096,256]{1,0:T(8,128)(2,1)S(1)} fusion(bf16[1,4096,1792]{2,1,0:T(8,128)(2,1)} %param.2, bf16[1,1792,256]{2,1,0:T(8,128)(2,1)S(1)} %copy-done), kind=kOutput, calls=%fused_computation.8 | convolution fusion | flops 3759144960 | bytes 17694720 | tf_op jit(solution)/shard_map/dot_general | solution.py:116
  16.9 55.3 %all_to_all.18 = bf16[8,512,256]{2,1,0:T(8,128)(2,1)S(1)} all-to-all(bf16[8,512,256]{2,1,0:T(8,128)(2,1)S(1)} %bitcast.48), channel_id=1, replica_groups=mesh['task'=4,'col'=8] {'col'}, dimensions={0} | all-to-all | bytes 4194304 | tf_op jit(solution)/shard_map/all_to_all | solution.py:110
  72.2 1.0 reduce_sum.33
  73.2 0.0 all-gather.5.cloned.1.call-update
  73.3 0.0 all-gather.7.cloned.1.call-start
  73.3 48.2 %all-gather.5.cloned.1.call-done = bf16[4096,256]{1,0:T(8,128)(2,1)} async-done(((bf16[512,256]{1,0:T(8,128)(2,1)}), bf16[4096,256]{1,0:T(8,128)(2,1)}) %all-gather.5.cloned.1.call-update) | async-done | bytes 2097168 | tf_op jit(solution)/shard_map/all_gather | solution.py:125
  121.5 2.2 multiply_reduce_fusion
  123.7 15.5 %fusion.11 = bf16[256,4096]{1,0:T(8,128)(2,1)S(1)} fusion(bf16[1,4096,1792]{2,1,0:T(8,128)(2,1)} %param.2, bf16[4096,256]{1,0:T(8,128)(2,1)} %all-gather.5.cloned.1.call-done, f32[256]{0:T(256)S(1)} %rsqrt.8), kind=kOutput, calls=%fused_computation.9 | convolution fusion | flops 7518158848 | bytes 18875392 | tf_op jit(solution)/shard_map/dot_general | solution.py:116
  139.2 0.2 copy.10
  139.4 50.7 %all_to_all.19 = bf16[8,512,256]{1,2,0:T(8,128)(2,1)S(1)} all-to-all(bf16[8,512,256]{1,2,0:T(8,128)(2,1)S(1)} %bitcast.46), channel_id=1, replica_groups=mesh['task'=4,'col'=8] {'col'}, dimensions={0} | all-to-all | bytes 4194304 | tf_op jit(solution)/shard_map/all_to_all | solution.py:110
  190.1 1.0 reduce_sum.35
  191.1 0.0 all-gather.7.cloned.1.call-update
  191.2 0.0 all-gather.9.cloned.1.call-start
  191.2 49.3 %all-gather.7.cloned.1.call-done = bf16[4096,256]{0,1:T(8,128)(2,1)} async-done(((bf16[512,256]{0,1:T(8,128)(2,1)}), bf16[4096,256]{0,1:T(8,128)(2,1)}) %all-gather.7.cloned.1.call-update) | async-done | bytes 2097168 | tf_op jit(solution)/shard_map/all_gather | solution.py:128
  240.6 0.0 copy-start.1
  240.6 0.0 all-gather.9.cloned.1.call-update
  240.6 0.3 all-gather.11.cloned.1.call-start
  240.9 3.1 fusion.26.gram_ref
  244.0 9.8 %inverse_factor.3 = f32[256,256]{1,0:T(8,128)S(1)} custom-call(f32[256,256]{1,0:T(8,128)S(1)} %fusion.26.gram_ref), custom_call_target="tpu_custom_call" | custom-call | tf_op jit(solution)/shard_map/inverse_factor/pallas_call | solution.py:98
  253.8 0.0 copy-done.1
  253.8 7.8 %fusion = f32[256,1792]{1,0:T(8,128)S(1)} fusion(bf16[4096,256]{0,1:T(8,128)(2,1)S(1)} %copy-done.1, bf16[1,4096,1792]{2,1,0:T(8,128)(2,1)} %param.2), kind=kOutput, calls=%fused_computation | convolution fusion | flops 3758096384 | bytes 18612224 | tf_op jit(solution)/shard_map/dot_general | solution.py:116
  261.6 2.6 convolution_convert_fusion.1
  264.2 0.0 all-gather.11.cloned.1.call-update
  264.2 34.4 %all-gather.9.cloned.1.call-done = bf16[4096,1024]{0,1:T(8,128)(2,1)} async-done(((bf16[4096,256]{0,1:T(8,128)(2,1)}), bf16[4096,1024]{0,1:T(8,128)(2,1)}) %all-gather.9.cloned.1.call-update) | async-done | bytes 8388624 | tf_op jit(solution)/shard_map/all_gather | solution.py:129
  298.6 15.9 %fusion.25.gram_ref = f32[1024,1024]{1,0:T(8,128)} fusion(bf16[4096,1024]{0,1:T(8,128)(2,1)} %all-gather.9.cloned.1.call-done), kind=kOutput, calls=%fused_computation.21 | convolution fusion | flops 8589934592 | bytes 12582912 | tf_op jit(solution)/shard_map/dot_general | solution.py:116
  314.5 64.8 %inverse_factor.2 = f32[1024,1024]{1,0:T(8,128)S(1)} custom-call(f32[1024,1024]{1,0:T(8,128)} %fusion.25.gram_ref), custom_call_target="tpu_custom_call" | custom-call | tf_op jit(solution)/shard_map/inverse_factor/pallas_call | solution.py:98
  379.3 9.3 %fusion.21 = bf16[1024,1024]{1,0:T(8,128)(2,1)S(1)} fusion(f32[1024,1024]{1,0:T(8,128)S(1)} %inverse_factor.2, bf16[4096,1024]{0,1:T(8,128)(2,1)} %all-gather.9.cloned.1.call-done, s32[]{:T(128)S(6)} %select_n.3), kind=kOutput, calls=%fused_computation.17 | convolution fusion | flops 12884901888 | bytes 8388612 | tf_op jit(solution)/shard_map/dot_general | solution.py:136
  388.6 0.0 all-gather.11.cloned.1.call-done
  388.7 7.4 %convolution_convert_fusion = bf16[1024,1792]{1,0:T(8,128)(2,1)} fusion(bf16[1024,1792]{1,0:T(8,128)(2,1)} %all-gather.11.cloned.1.call-done, bf16[1024,1024]{1,0:T(8,128)(2,1)S(1)} %fusion.21), kind=kOutput, calls=%fused_computation.11 | convolution fusion | flops 3759931392 | bytes 9437184 | tf_op jit(solution)/shard_map/dot_general | solution.py:116
  (1 shorter events, 0.0 us)
Async XLA Ops:
  6.5 1.2 copy-start
  6.5 115.0 %all-gather.5.cloned.1.call-start = ((), (), s32[]{:S(2)}) async-start(), calls=%async_computation.2 | async-start | bytes 2359296 | tf_op jit(solution)/shard_map/all_gather | solution.py:125
  73.3 167.3 %all-gather.7.cloned.1.call-start = ((), (), s32[]{:S(2)}) async-start(), calls=%async_computation.3 | async-start | bytes 2359296 | tf_op jit(solution)/shard_map/all_gather | solution.py:128
  191.2 107.5 %all-gather.9.cloned.1.call-start = ((), (), s32[]{:S(2)}) async-start(), calls=%async_computation.4 | async-start | bytes 10485760 | tf_op jit(solution)/shard_map/all_gather | solution.py:129
  240.6 13.2 %copy-start.1 = (bf16[4096,256]{0,1:T(8,128)(2,1)S(1)}, bf16[4096,256]{0,1:T(8,128)(2,1)}, u32[]{:S(2)}) copy-start(bf16[4096,256]{0,1:T(8,128)(2,1)} %all-gather.7.cloned.1.call-done) | copy-start | bytes 6291460
  240.6 148.1 %all-gather.11.cloned.1.call-start = ((), (), s32[]{:S(2)}) async-start(), calls=%async_computation.5 | async-start | bytes 4587520 | tf_op jit(solution)/shard_map/all_gather | solution.py:132
Sparse Core Ops, SparseCore 0:
  73.4 48.1 all-gather.4
  191.3 49.2 all-gather.6
  242.1 56.4 all-gather.8
  300.0 31.5 all-gather.10

commit v3 on v2

--- a/solution.py
+++ b/solution.py
@@ -8,6 +8,7 @@
 BLOCK = 128
 SUB = 8
 STRIDE = 4
+HALVES = 2
 CHUNK = 256
 
 
@@ -106,10 +107,19 @@
 
 def summed(partial):
     devices = lax.axis_size("col")
-    rows = partial.shape[0] // devices
-    parts = lax.all_to_all(partial.astype(jnp.bfloat16), "col", 0, 0, tiled=True)
-    parts = parts.reshape(devices, rows, partial.shape[1])
-    return jnp.sum(parts.astype(jnp.float32), axis=0).astype(jnp.bfloat16)
+    width = partial.shape[1]
+    partial = partial.astype(jnp.bfloat16).reshape(devices, HALVES, -1, width)
+    halves = []
+    total = None
+    for half in range(HALVES):
+        mine = partial[:, half]
+        if half:
+            mine, total = lax.optimization_barrier((mine, total))
+            halves[-1] = lax.all_gather(total, "col", axis=0)
+        parts = lax.all_to_all(mine, "col", 0, 0, tiled=True)
+        total = jnp.sum(parts.astype(jnp.float32), axis=0).astype(jnp.bfloat16)
+        halves.append(lax.all_gather(total, "col", axis=0))
+    return jnp.stack(halves, axis=1).reshape(-1, width)
 
 
 def product(lhs, rhs, contract):
@@ -122,10 +132,10 @@
 
 def shards(deltas, sketch):
     delta = deltas[0]
-    first = lax.all_gather(summed(product(delta, sketch[0], INNER)), "col", axis=0, tiled=True)
+    first = summed(product(delta, sketch[0], INNER))
     norms = jnp.sum(jnp.square(first.astype(jnp.float32)), axis=0, keepdims=True)
     across = (product(delta, first, ROWS) * lax.rsqrt(norms)).astype(jnp.bfloat16)
-    ranged = lax.all_gather(summed(product(delta, across, INNER)), "col", axis=0, tiled=True)
+    ranged = summed(product(delta, across, INNER))
     joined = lax.all_gather(ranged, "task", axis=1, tiled=True)
     inverse = inverse_factor(product(ranged, ranged, ROWS))
     coeffs = dot_exact(inverse, product(ranged, delta, ROWS)).astype(jnp.bfloat16)

time: 405 us -> 471 us (1.16)
  waiting for transfers between devices: 132 us -> 236 us
  blocking collectives: 106 us -> 32.8 us
  local copies, waits for them, and re-layouts: 1.38 us -> 21.2 us
  starting transfers between devices: 0.38 us -> 11.9 us
  other arithmetic: 4.25 us -> 10 us
    all_to_all x0 -> x3, waiting for transfers between devices: none -> 79 us  [summed(): parts = lax.all_to_all(mine, 'col', 0, 0, tiled=True)]
    all_to_all x2 -> x1, blocking collectives: 106 us -> 32.8 us  [summed(): parts = lax.all_to_all(mine, 'col', 0, 0, tiled=True)]
    all_gather x2 -> x4, waiting for transfers between devices: 97.6 us -> 120 us  [the longest x2 82.1 us: summed(): halves.append(lax.all_gather(total, 'col', axis=0))]
    unnamed x4 -> x18, local copies, waits for them, and re-layouts: 1.18 us -> 12.6 us
    all_to_all x0 -> x3, starting transfers between devices: none -> 11.4 us  [summed(): parts = lax.all_to_all(mine, 'col', 0, 0, tiled=True)]
    another operation x0 -> x2, other arithmetic: none -> 4.94 us  [summed(): return jnp.stack(halves, axis=1).reshape(-1, width)]
  transfers between devices with their start and end apart: 4 -> 9, of which waited for: 3 -> 8; matrix products, arithmetic and copies ran while one was open for 10% -> 9% of each run, Pallas kernels for 19% -> 16%
where the time goes in v3:
time: 471 us; the launch traced here: 468 us
  waiting for transfers between devices  236 us (50%)
  Pallas kernels  74.6 us (16%)
  matrix products  67.7 us (14%)
  blocking collectives  32.8 us (7%)
  local copies, waits for them, and re-layouts  21.2 us (5%)
  between operations  13.8 us (3%)
  starting transfers between devices  11.9 us (3%)
  other arithmetic  10 us (2%)
    all_gather x2, waiting for transfers between devices, summed(): halves.append(lax.all_gather(total, 'col', axis=0))  82.1 us
    all_to_all x3, waiting for transfers between devices, summed(): parts = lax.all_to_all(mine, 'col', 0, 0, tiled=True)  79 us
    pallas_call x2, Pallas kernels, inverse_factor(): pl.pallas_call(inverse_factor_kernel, out_shape=jax.ShapeDtypeStruct(gram...  74.6 us
    dot_general x6, matrix products, product(): lax.dot_general(lhs, rhs, (contract, ((), ())), preferred_element_type=jn...  56.7 us
    all_gather x2, waiting for transfers between devices, summed(): halves[-1] = lax.all_gather(total, 'col', axis=0)  37.6 us
    all_gather x1, waiting for transfers between devices, shards(): joined = lax.all_gather(ranged, 'task', axis=1, tiled=True)  35.5 us
    all_to_all x1, blocking collectives, summed(): parts = lax.all_to_all(mine, 'col', 0, 0, tiled=True)  32.8 us
    unnamed x18, local copies, waits for them, and re-layouts  12.6 us
  transfers between devices with their start and end apart: 9, of which 8 were waited for; matrix products, arithmetic and copies ran while one was open for 9% of the time, Pallas kernels for 16%

profile of v3, /device:TPU:0, one launch (start us, length us, event | category | flops | bytes accessed | tf_op | source)
XLA Modules:
  0.0 467.6 jit_solution(279892197389287648)
XLA Ops:
  6.5 1.2 copy-done
  7.7 9.2 %fusion.8 = bf16[4096,256]{1,0:T(8,128)(2,1)S(1)} fusion(bf16[1,4096,1792]{2,1,0:T(8,128)(2,1)} %param.2, bf16[1,1792,256]{2,1,0:T(8,128)(2,1)S(1)} %copy-done), kind=kOutput, calls=%fused_computation.8 | convolution fusion | flops 3759144960 | bytes 17694720 | tf_op jit(solution)/shard_map/dot_general | solution.py:126
  16.9 1.1 slice_bitcast_fusion
  18.0 32.8 %all_to_all.20 = bf16[8,256,256]{2,1,0:T(8,128)(2,1)S(1)} all-to-all(bf16[8,256,256]{2,1,0:T(8,128)(2,1)S(1)} %get-tuple-element.15), channel_id=1, replica_groups=mesh['task'=4,'col'=8] {'col'}, dimensions={0} | all-to-all | bytes 2097152 | tf_op jit(solution)/shard_map/all_to_all | solution.py:119
  50.8 0.8 reduce_sum.57
  51.6 3.6 all-to-all-start.1
  55.2 0.0 all-gather.15.cloned.1.call-start
  55.3 0.7 all-gather.15.cloned.1.call-update
  55.9 0.0 all-gather.17.cloned.1.call-start
  56.0 29.0 %all-to-all-done.1 = bf16[8,256,256]{2,1,0:T(8,128)(2,1)S(1)} async-done(((bf16[8,256,256]{2,1,0:T(8,128)(2,1)}), bf16[8,256,256]{2,1,0:T(8,128)(2,1)S(1)}, u32[]{:S(2)}, u32[]{:S(2)}) %all-to-all-start.1) | async-done | bytes 1048608 | tf_op jit(solution)/shard_map/all_to_all | solution.py:119
  85.0 0.8 reduce_sum.58
  85.8 0.0 all-gather.17.cloned.1.call-update
  85.8 18.9 %all-gather.15.cloned.1.call-done = bf16[2048,256]{1,0:T(8,128)(2,1)} async-done(((bf16[256,256]{1,0:T(8,128)(2,1)}), bf16[2048,256]{1,0:T(8,128)(2,1)}) %all-gather.15.cloned.1.call-update) | async-done | bytes 1048592 | tf_op jit(solution)/shard_map/all_gather | solution.py:118
  104.7 41.1 %all-gather.17.cloned.1.call-done = bf16[2048,256]{1,0:T(8,128)(2,1)} async-done(((bf16[256,256]{1,0:T(8,128)(2,1)}), bf16[2048,256]{1,0:T(8,128)(2,1)}) %all-gather.17.cloned.1.call-update) | async-done | bytes 1048592 | tf_op jit(solution)/shard_map/all_gather | solution.py:121
  145.9 1.9 pad_maximum_fusion
  147.8 0.3 copy-done.5
  148.0 0.6 multiply_reduce_fusion
  148.6 16.1 %fusion.14 = bf16[4096,256]{0,1:T(8,128)(2,1)} fusion(bf16[1,4096,1792]{2,1,0:T(8,128)(2,1)} %param.2, bf16[4096,256]{1,0:T(8,128)(2,1)S(1)} %bitcast.69, f32[256]{0:T(256)S(1)} %rsqrt.8), kind=kOutput, calls=%fused_computation.10 | convolution fusion | flops 7518158848 | bytes 18875392 | tf_op jit(solution)/shard_map/dot_general | solution.py:126
  164.8 3.3 reshape.18
  168.1 4.2 fusion.28
  172.2 5.9 %copy.7 = bf16[8,1,256,256]{3,2,0,1:T(8,128)(2,1)} copy(bf16[8,1,256,256]{2,1,0,3:T(2,128)(2,1)} %get-tuple-element.13) | data formatting | bytes 2097152
  178.2 4.2 all-to-all-start.2
  182.4 3.7 copy.6
  186.2 20.8 %all-to-all-done.2 = bf16[8,256,256]{2,1,0:T(8,128)(2,1)} async-done(((bf16[8,256,256]{2,1,0:T(8,128)(2,1)}), bf16[8,256,256]{2,1,0:T(8,128)(2,1)}, u32[]{:S(2)}, u32[]{:S(2)}) %all-to-all-start.2) | async-done | bytes 1048608 | tf_op jit(solution)/shard_map/all_to_all | solution.py:119
  206.9 2.1 reduce_sum.60
  209.0 3.6 all-to-all-start.3
  212.6 0.0 all-gather.19.cloned.1.call-start
  212.6 0.7 all-gather.19.cloned.1.call-update
  213.3 0.0 all-gather.21.cloned.1.call-start
  213.4 29.2 %all-to-all-done.3 = bf16[8,256,256]{2,1,0:T(8,128)(2,1)S(1)} async-done(((bf16[8,256,256]{2,1,0:T(8,128)(2,1)}), bf16[8,256,256]{2,1,0:T(8,128)(2,1)S(1)}, u32[]{:S(2)}, u32[]{:S(2)}) %all-to-all-start.3) | async-done | bytes 1048608 | tf_op jit(solution)/shard_map/all_to_all | solution.py:119
  242.5 0.8 reduce_sum.61
  243.4 0.3 all-gather.11.cloned.1.call-start
  243.7 18.7 %all-gather.19.cloned.1.call-done = bf16[2048,256]{1,0:T(8,128)(2,1)} async-done(((bf16[256,256]{1,0:T(8,128)(2,1)}), bf16[2048,256]{1,0:T(8,128)(2,1)}) %all-gather.19.cloned.1.call-update) | async-done | bytes 1048592 | tf_op jit(solution)/shard_map/all_gather | solution.py:118
  262.3 41.0 %all-gather.21.cloned.1.call-done = bf16[2048,256]{1,0:T(8,128)(2,1)} async-done(((bf16[256,256]{1,0:T(8,128)(2,1)}), bf16[2048,256]{1,0:T(8,128)(2,1)}) %all-gather.21.cloned.1.call-update) | async-done | bytes 1048592 | tf_op jit(solution)/shard_map/all_gather | solution.py:121
  303.3 3.1 pad_maximum_fusion.1
  306.4 0.0 all-gather.13.cloned.1.call-start
  306.5 1.1 copy-done.6
  307.6 0.3 copy-done.7
  307.9 0.7 convolution_bitcast_fusion.gram_ref
  308.7 9.8 %inverse_factor.3 = f32[256,256]{1,0:T(8,128)S(1)} custom-call(f32[256,256]{1,0:T(8,128)S(1)} %convolution_bitcast_fusion.gram_ref), custom_call_target="tpu_custom_call" | custom-call | tf_op jit(solution)/shard_map/inverse_factor/pallas_call | solution.py:99
  318.5 8.1 %fusion = f32[256,1792]{1,0:T(8,128)S(1)} fusion(bf16[4096,256]{1,0:T(8,128)(2,1)S(1)} %bitcast.62, bf16[1,4096,1792]{2,1,0:T(8,128)(2,1)} %param.2), kind=kOutput, calls=%fused_computation | convolution fusion | flops 3758096384 | bytes 18612224 | tf_op jit(solution)/shard_map/dot_general | solution.py:126
  326.6 2.6 convolution_convert_fusion.1
  329.2 35.5 %all-gather.11.cloned.1.call-done = bf16[4096,1024]{1,0:T(8,128)(2,1)} async-done(((bf16[4096,256]{1,0:T(8,128)(2,1)}), bf16[4096,1024]{1,0:T(8,128)(2,1)}) %all-gather.11.cloned.1.call-update) | async-done | bytes 8388624 | tf_op jit(solution)/shard_map/all_gather | solution.py:139
  364.7 15.1 %fusion.29.gram_ref = f32[1024,1024]{1,0:T(8,128)} fusion(bf16[4096,1024]{1,0:T(8,128)(2,1)} %all-gather.11.cloned.1.call-done), kind=kOutput, calls=%fused_computation.27 | convolution fusion | flops 8589934592 | bytes 12582912 | tf_op jit(solution)/shard_map/dot_general | solution.py:126
  379.8 64.8 %inverse_factor.2 = f32[1024,1024]{1,0:T(8,128)S(1)} custom-call(f32[1024,1024]{1,0:T(8,128)} %fusion.29.gram_ref), custom_call_target="tpu_custom_call" | custom-call | tf_op jit(solution)/shard_map/inverse_factor/pallas_call | solution.py:99
  444.6 8.4 %fusion.24 = bf16[1024,1024]{1,0:T(8,128)(2,1)S(1)} fusion(f32[1024,1024]{1,0:T(8,128)S(1)} %inverse_factor.2, bf16[4096,1024]{1,0:T(8,128)(2,1)} %all-gather.11.cloned.1.call-done, s32[]{:T(128)S(6)} %select_n.3), kind=kOutput, calls=%fused_computation.19 | convolution fusion | flops 12884901888 | bytes 8388612 | tf_op jit(solution)/shard_map/dot_general | solution.py:146
  453.0 0.0 all-gather.13.cloned.1.call-done
  453.0 7.5 %convolution_convert_fusion = bf16[1024,1792]{1,0:T(8,128)(2,1)} fusion(bf16[1024,1792]{1,0:T(8,128)(2,1)} %all-gather.13.cloned.1.call-done, bf16[1024,1024]{1,0:T(8,128)(2,1)S(1)} %fusion.24), kind=kOutput, calls=%fused_computation.12 | convolution fusion | flops 3759931392 | bytes 9437184 | tf_op jit(solution)/shard_map/dot_general | solution.py:126
  (16 shorter events, 0.1 us)
Async XLA Ops:
  6.5 1.2 copy-start
  51.6 33.4 %all-to-all-start.1 = ((bf16[8,256,256]{2,1,0:T(8,128)(2,1)}), bf16[8,256,256]{2,1,0:T(8,128)(2,1)S(1)}, u32[]{:S(2)}, u32[]{:S(2)}) async-start(bf16[8,256,256]{2,1,0:T(8,128)(2,1)} %get-tuple-element.10), calls=%async_computation.1 | async-start | bytes 2097152 | tf_op jit(solution)/shard_map/all_to_all | solution.py:119
  55.2 49.5 %all-gather.15.cloned.1.call-start = ((), (), s32[]{:S(2)}) async-start(), calls=%async_computation.6 | async-start | bytes 1179648 | tf_op jit(solution)/shard_map/all_gather | solution.py:118
  55.9 89.9 %all-gather.17.cloned.1.call-start = ((), (), s32[]{:S(2)}) async-start(), calls=%async_computation.7 | async-start | bytes 1179648 | tf_op jit(solution)/shard_map/all_gather | solution.py:121
  145.9 1.9 copy-start.4
  145.9 2.2 copy-start.5
  172.2 10.2 %copy-start.3 = (bf16[8,1,256,256]{2,1,0,3:T(2,128)(2,1)S(1)}, bf16[8,1,256,256]{2,1,0,3:T(2,128)(2,1)}, u32[]{:S(2)}) copy-start(bf16[8,1,256,256]{2,1,0,3:T(2,128)(2,1)} %get-tuple-element.14) | copy-start | bytes 3145732
  178.2 28.8 %all-to-all-start.2 = ((bf16[8,256,256]{2,1,0:T(8,128)(2,1)}), bf16[8,256,256]{2,1,0:T(8,128)(2,1)}, u32[]{:S(2)}, u32[]{:S(2)}) async-start(bf16[8,256,256]{2,1,0:T(8,128)(2,1)} %bitcast.64), calls=%async_computation.2 | async-start | bytes 2097152 | tf_op jit(solution)/shard_map/all_to_all | solution.py:119
  209.0 33.5 %all-to-all-start.3 = ((bf16[8,256,256]{2,1,0:T(8,128)(2,1)}), bf16[8,256,256]{2,1,0:T(8,128)(2,1)S(1)}, u32[]{:S(2)}, u32[]{:S(2)}) async-start(bf16[8,256,256]{2,1,0:T(8,128)(2,1)} %bitcast.63), calls=%async_computation.3 | async-start | bytes 2097152 | tf_op jit(solution)/shard_map/all_to_all | solution.py:119
  212.6 49.8 %all-gather.19.cloned.1.call-start = ((), (), s32[]{:S(2)}) async-start(), calls=%async_computation.8 | async-start | bytes 1179648 | tf_op jit(solution)/shard_map/all_gather | solution.py:118
  213.3 90.0 %all-gather.21.cloned.1.call-start = ((), (), s32[]{:S(2)}) async-start(), calls=%async_computation.9 | async-start | bytes 1179648 | tf_op jit(solution)/shard_map/all_gather | solution.py:121
  243.4 121.4 %all-gather.11.cloned.1.call-start = ((), (), s32[]{:S(2)}) async-start(), calls=%async_computation.4 | async-start | bytes 10485760 | tf_op jit(solution)/shard_map/all_gather | solution.py:139
  306.4 1.2 copy-start.6
  306.4 1.5 copy-start.7
  306.4 146.6 %all-gather.13.cloned.1.call-start = ((), (), s32[]{:S(2)}) async-start(), calls=%async_computation.5 | async-start | bytes 4587520 | tf_op jit(solution)/shard_map/all_gather | solution.py:142
  307.9 10.5 %copy-start.2 = (bf16[8,2,256,256]{3,2,1,0:T(8,128)(2,1)S(1)}, bf16[8,2,256,256]{3,2,1,0:T(8,128)(2,1)}, u32[]{:S(2)}) copy-start(bf16[8,2,256,256]{3,2,1,0:T(8,128)(2,1)} %pad_maximum_fusion.1) | copy-start | bytes 6291460
  453.0 7.5 %copy-start.1 = (bf16[1,1792,256]{2,1,0:T(8,128)(2,1)S(1)}, bf16[1,1792,256]{2,1,0:T(8,128)(2,1)}, u32[]{:S(2)}) copy-start(bf16[1,1792,256]{2,1,0:T(8,128)(2,1)} %param.3) | copy-start | bytes 2752516
Sparse Core Ops, SparseCore 0:
  58.1 46.5 all-gather.14
  106.8 38.9 all-gather.16
  215.5 46.7 all-gather.18
  264.3 38.9 all-gather.20
  306.5 58.1 all-gather.10
  366.2 31.4 all-gather.12
